TPU v7x, 32 devices: a whole 2x2x4 slice. The times are simulated.
32 devices in a mesh: row: 8 (over y, x, core), col: 4 (over z).
Axes of the slice: x: 2, y: 2, z: 4, core: 2. Of those that a mesh axis runs over, the one named last changes fastest.
Arguments:
- field: float32 [64, 128, 512], P(None, 'row', 'col'), may hold values from -4 to 6.5, as said below
- conductivity: float32 [64, 128, 512], P(None, 'row', 'col'), may hold values from 35 to 5600, as said below
Outputs:
- new_field: float32 [64, 128, 512], P(None, 'row', 'col')
Inputs may be any that keep to these rules, and one draw needn't show every extreme that they name: `field`: finite values. `conductivity`: positive in every cell.
All inputs are finite; a program needn't handle non-finite values.
Results may differ from a plain program's by a relative error of at most 0.0003.
Values sent between devices are 32-bit elements; how exact they have to be, the bound alone decides.
A program may use at most 64 MiB of HBM per device.

v0:
```python
import jax
import jax.numpy as jnp
from jax import lax
from jax.sharding import PartitionSpec as P

z_weight = 0.02


def padded_2(block, sides, width):
    for axis, dim in sides:
        count = lax.axis_size(axis)
        forward = [(i, i + 1) for i in range(count - 1)]
        backward = [(target, source) for source, target in forward]
        low = lax.ppermute(
            lax.slice_in_dim(block, block.shape[dim] - width, None, axis=dim), axis, forward
        )
        high = lax.ppermute(lax.slice_in_dim(block, 0, width, axis=dim), axis, backward)
        block = jnp.concatenate([low, block, high], axis=dim)
    return block


def neighbour(values, line_axis, offset):
    length = values.shape[line_axis]
    widths = [(0, 0)] * values.ndim
    widths[line_axis] = (1, 1)
    padded = jnp.pad(values, widths)
    return lax.slice_in_dim(padded, 1 + offset, 1 + offset + length, axis=line_axis)


def shifted(values, line_axis, stride, fill):
    length = values.shape[line_axis]
    pad_shape = list(values.shape)
    pad_shape[line_axis] = abs(stride)
    padding = jnp.full(pad_shape, fill, values.dtype)
    if stride > 0:
        kept_part = lax.slice_in_dim(values, 0, length - stride, axis=line_axis)
        return jnp.concatenate((padding, kept_part), axis=line_axis)
    kept_part = lax.slice_in_dim(values, -stride, length, axis=line_axis)
    return jnp.concatenate((kept_part, padding), axis=line_axis)


def reduce_lines(below_diag, diagonal, above_diag, columns, line_axis):
    length = diagonal.shape[line_axis]
    stride = 1
    while stride < length:
        left_factor = -below_diag / shifted(diagonal, line_axis, stride, 1.0)
        right_factor = -above_diag / shifted(diagonal, line_axis, -stride, 1.0)
        new_diag = (
            diagonal
            + left_factor * shifted(above_diag, line_axis, stride, 0.0)
            + right_factor * shifted(below_diag, line_axis, -stride, 0.0)
        )
        new_below = left_factor * shifted(below_diag, line_axis, stride, 0.0)
        new_above = right_factor * shifted(above_diag, line_axis, -stride, 0.0)
        columns = [
            column
            + left_factor * shifted(column, line_axis, stride, 0.0)
            + right_factor * shifted(column, line_axis, -stride, 0.0)
            for column in columns
        ]
        below_diag, diagonal, above_diag = (new_below, new_diag, new_above)
        stride = stride * 2
    return (diagonal, columns)


def local_spikes(below_diag, above_diag, right_side, line_axis):
    length = right_side.shape[line_axis]
    position = lax.broadcasted_iota(jnp.int32, right_side.shape, line_axis)
    first_row = position == 0
    last_row = position == length - 1
    diagonal = 1.0 - below_diag - above_diag
    left_column = jnp.where(first_row, below_diag, 0.0)
    right_column = jnp.where(last_row, above_diag, 0.0)
    below_inner = jnp.where(first_row, 0.0, below_diag)
    above_inner = jnp.where(last_row, 0.0, above_diag)
    diagonal, columns = reduce_lines(
        below_inner, diagonal, above_inner, [right_side, left_column, right_column], line_axis
    )
    local_part = columns[0] / diagonal
    left_spike = columns[1] / diagonal
    right_spike = columns[2] / diagonal
    planes = []
    for member in (local_part, left_spike, right_spike):
        planes.append(lax.index_in_dim(member, 0, line_axis, keepdims=False))
        planes.append(lax.index_in_dim(member, length - 1, line_axis, keepdims=False))
    return (local_part, left_spike, right_spike, jnp.stack(planes)[None])


def join_spikes(gathered, local_part, left_spike, right_spike, line_axis, index_here, group_size):
    columns_in = tuple((gathered[:, member] for member in range(6)))
    zero_plane = jnp.zeros_like(columns_in[0][0])

    def forward(state_now, inputs):
        spike_prev, carry_prev = state_now
        head_local, tail_local, head_left, tail_left, head_right, tail_right = inputs
        pivot_here = 1.0 - head_left * spike_prev
        ratio_here = head_right / pivot_here
        first_here = (head_local - head_left * carry_prev) / pivot_here
        spike_next = tail_right + tail_left * spike_prev * ratio_here
        carry_next = tail_local - tail_left * carry_prev + tail_left * spike_prev * first_here
        return ((spike_next, carry_next), (ratio_here, spike_next, first_here, carry_next))

    unused, outputs = lax.scan(forward, (zero_plane, zero_plane), columns_in)

    def backward(next_head, inputs):
        ratio_here, spike_here, first_here, last_here = inputs
        head_value = first_here - ratio_here * next_head
        tail_value = last_here - spike_here * next_head
        return (head_value, (head_value, tail_value))

    unused_last, ends = lax.scan(backward, zero_plane, outputs, reverse=True)
    first_values, last_values = ends
    left_value = lax.dynamic_index_in_dim(
        last_values, jnp.maximum(index_here - 1, 0), 0, keepdims=False
    ) * (index_here > 0).astype(jnp.float32)
    right_value = lax.dynamic_index_in_dim(
        first_values, jnp.minimum(index_here + 1, group_size - 1), 0, keepdims=False
    ) * (index_here < group_size - 1).astype(jnp.float32)
    return (
        local_part
        - jnp.expand_dims(left_value, line_axis) * left_spike
        - jnp.expand_dims(right_value, line_axis) * right_spike
    )


def on_device(field, conductivity):
    stacked = jnp.stack((field, conductivity))
    padded = padded_2(stacked, (("row", 2), ("col", 3)), 1)
    field_pad = padded[0]
    cond_pad = padded[1]
    west_cond = cond_pad[:, :-2, 1:-1]
    east_cond = cond_pad[:, 2:, 1:-1]
    south_cond = cond_pad[:, 1:-1, :-2]
    north_cond = cond_pad[:, 1:-1, 2:]
    west_field = field_pad[:, :-2, 1:-1]
    east_field = field_pad[:, 2:, 1:-1]
    south_field = field_pad[:, 1:-1, :-2]
    north_field = field_pad[:, 1:-1, 2:]
    east_xdir = 0.5 * 1.0 * (conductivity + east_cond)
    west_xdir = 0.5 * 1.0 * (conductivity + west_cond)
    east_ydir = 0.5 * 1.0 * (conductivity + north_cond)
    west_ydir = 0.5 * 1.0 * (conductivity + south_cond)
    flux_xdir = east_xdir * (east_field - field) - west_xdir * (field - west_field)
    flux_ydir = east_ydir * (north_field - field) - west_ydir * (field - south_field)
    east_zdir = 0.5 * z_weight * (conductivity + neighbour(conductivity, 0, 1))
    west_zdir = 0.5 * z_weight * (conductivity + neighbour(conductivity, 0, -1))
    flux_zdir = east_zdir * (neighbour(field, 0, 1) - field) - west_zdir * (
        field - neighbour(field, 0, -1)
    )
    explicit = flux_xdir + flux_ydir + flux_zdir
    local_part, left_spike, right_spike, planes = local_spikes(-west_xdir, -east_xdir, explicit, 1)
    gathered = lax.all_gather(planes, "row", axis=0, tiled=True)
    delta_xdir = join_spikes(
        gathered,
        local_part,
        left_spike,
        right_spike,
        1,
        lax.axis_index("row"),
        lax.axis_size("row"),
    )
    local_part, left_spike, right_spike, planes = local_spikes(
        -west_ydir, -east_ydir, delta_xdir, 2
    )
    gathered = lax.all_gather(planes, "col", axis=0, tiled=True)
    delta_ydir = join_spikes(
        gathered,
        local_part,
        left_spike,
        right_spike,
        2,
        lax.axis_index("col"),
        lax.axis_size("col"),
    )
    return field + delta_ydir


def solution(mesh):
    in_specs = (P(None, "row", "col"), P(None, "row", "col"))
    out_specs = P(None, "row", "col")
    return jax.shard_map(
        on_device, mesh=mesh, in_specs=in_specs, out_specs=out_specs, check_vma=False
    )
```

profile of v0, /device:TPU:0, one launch (start us, length us, event | category | flops | bytes accessed | tf_op | source)
XLA Modules:
  0.0 144.2 jit_solution(15308119017377806291)
XLA Ops:
  6.5 2.5 %fusion.59 = (f32[64,16,128]{2,0,1:T(8,128)}, f32[1,64,16,128]{3,1,2,0:T(8,128)S(1)}, f32[1,64,16,128]{3,1,2,0:T(8,128)S(1)}, f32[64,16,128]{2,0,1:T(8,128)}) fusion(f32[64,16,128]{2,1,0:T(8,128)} %param.10, f32[64,16,128]{2,1,0:T(8,128)} %param.11), kind=kLoop, calls=%fused_computation.241 | loop fusion | bytes 3145728 | tf_op args[0]
  10.4 3.0 %collective-permute-start = (f32[2,64,1,128]{3,1,2,0:T(8,128)S(1)}, f32[2,64,1,128]{3,1,2,0:T(8,128)S(1)}, u32[]{:S(2)}, u32[]{:S(2)}) collective-permute-start(f32[2,64,1,128]{3,1,2,0:T(8,128)S(1)} %get-tuple-element.850), channel_id=1, source_target_pairs={{0,4},{4,8},{8,12},{12,16},{16,20},{20,24},{24,28},{1,5},{5,9},{9,... | collective-permute-start | bytes 196616 | tf_op jit(solution)/shard_map/ppermute | solution.py:14
  17.6 6.2 %collective-permute-start.2 = (f32[2,64,18,1]{1,0,3,2:T(2,128)S(1)}, f32[2,64,18,1]{1,0,3,2:T(2,128)}, u32[]{:S(2)}, u32[]{:S(2)}) collective-permute-start(f32[2,64,18,1]{1,0,3,2:T(2,128)S(1)} %copy.303), channel_id=1, source_target_pairs={{0,1},{1,2},{2,3},{4,5},{5,6},{6,7},{8,9},{9,10},{10,11},{12,13},{... | collective-permute-start | bytes 27656 | tf_op jit(solution)/shard_map/ppermute | solution.py:14
  45.8 23.3 %all-gather.4.cloned.1.call-done = f32[48,64,128]{2,1,0:T(8,128)} async-done(((f32[6,64,128]{2,1,0:T(8,128)}), f32[48,64,128]{2,1,0:T(8,128)}) %all-gather.4.cloned.1.call-update) | async-done | bytes 1572880 | tf_op jit(solution)/shard_map/all_gather | solution.py:152
  69.1 2.4 %slice_bitcast_fusion.2 = (f32[8,64,128]{2,1,0:T(8,128)S(1)}, f32[8,64,128]{2,1,0:T(8,128)S(1)}, f32[8,64,128]{2,1,0:T(8,128)}, f32[8,64,128]{2,1,0:T(8,128)}, f32[8,64,128]{2,1,0:T(8,128)}, /*index=5*/f32[8,64,128]{2,1,0:T(8,128)}) fusion(f32[8,6,64,128]{3,2,1,0:T(8,128)} %bitcast.281), kind=kLoop, calls=%fused_computation.177 | loop fusion | bytes 3145728 | tf_op jit(solution)/shard_map/squeeze | solution.py:90
  74.4 12.1 %while.80 = (s32[]{:T(128)}, f32[64,128]{1,0:T(8,128)S(1)}, f32[64,128]{1,0:T(8,128)S(1)}, f32[8,64,128]{2,1,0:T(8,128)}, f32[8,64,128]{2,1,0:T(8,128)}, /*index...) while((s32[]{:T(128)}, f32[64,128]{1,0:T(8,128)S(1)}, ...), condition=%wide.region_1.2_spmd.clone, body=%wide.region_0.1_spmd.clone.sunk | while | flops 122883 | bytes 458915 | solution.py:103
  74.4 1.6 %bitcast_dynamic-update-slice_fusion.16 = (f32[8,64,128]{2,1,0:T(8,128)}, f32[64,128]{1,0:T(8,128)S(1)}, f32[8,64,128]{2,1,0:T(8,128)}, f32[8,64,128]{2,1,0:T(8,...) fusion(f32[8,64,128]{2,1,0:T(8,128)} %get-tuple-element.1309, s32[]{:T(128)S(6)} %copy.408, ...), kind=kLoop, calls=%fused_computation.clone.1 | loop fusion | flops 122880 | bytes 458757 | tf_op jit(solution)/shard_map/while/body/jit(dynamic_update_index_in_dim)/dynamic_update_slice | solution.py:103
  76.0 1.5 %bitcast_dynamic-update-slice_fusion.16 = (f32[8,64,128]{2,1,0:T(8,128)}, f32[64,128]{1,0:T(8,128)S(1)}, f32[8,64,128]{2,1,0:T(8,128)}, f32[8,64,128]{2,1,0:T(8,...) fusion(f32[8,64,128]{2,1,0:T(8,128)} %get-tuple-element.1309, s32[]{:T(128)S(6)} %copy.408, ...), kind=kLoop, calls=%fused_computation.clone.1 | loop fusion | flops 122880 | bytes 458757 | tf_op jit(solution)/shard_map/while/body/jit(dynamic_update_index_in_dim)/dynamic_update_slice | solution.py:103
  77.5 1.5 %bitcast_dynamic-update-slice_fusion.16 = (f32[8,64,128]{2,1,0:T(8,128)}, f32[64,128]{1,0:T(8,128)S(1)}, f32[8,64,128]{2,1,0:T(8,128)}, f32[8,64,128]{2,1,0:T(8,...) fusion(f32[8,64,128]{2,1,0:T(8,128)} %get-tuple-element.1309, s32[]{:T(128)S(6)} %copy.408, ...), kind=kLoop, calls=%fused_computation.clone.1 | loop fusion | flops 122880 | bytes 458757 | tf_op jit(solution)/shard_map/while/body/jit(dynamic_update_index_in_dim)/dynamic_update_slice | solution.py:103
  79.0 1.5 %bitcast_dynamic-update-slice_fusion.16 = (f32[8,64,128]{2,1,0:T(8,128)}, f32[64,128]{1,0:T(8,128)S(1)}, f32[8,64,128]{2,1,0:T(8,128)}, f32[8,64,128]{2,1,0:T(8,...) fusion(f32[8,64,128]{2,1,0:T(8,128)} %get-tuple-element.1309, s32[]{:T(128)S(6)} %copy.408, ...), kind=kLoop, calls=%fused_computation.clone.1 | loop fusion | flops 122880 | bytes 458757 | tf_op jit(solution)/shard_map/while/body/jit(dynamic_update_index_in_dim)/dynamic_update_slice | solution.py:103
  80.5 1.5 %bitcast_dynamic-update-slice_fusion.16 = (f32[8,64,128]{2,1,0:T(8,128)}, f32[64,128]{1,0:T(8,128)S(1)}, f32[8,64,128]{2,1,0:T(8,128)}, f32[8,64,128]{2,1,0:T(8,...) fusion(f32[8,64,128]{2,1,0:T(8,128)} %get-tuple-element.1309, s32[]{:T(128)S(6)} %copy.408, ...), kind=kLoop, calls=%fused_computation.clone.1 | loop fusion | flops 122880 | bytes 458757 | tf_op jit(solution)/shard_map/while/body/jit(dynamic_update_index_in_dim)/dynamic_update_slice | solution.py:103
  82.0 1.5 %bitcast_dynamic-update-slice_fusion.16 = (f32[8,64,128]{2,1,0:T(8,128)}, f32[64,128]{1,0:T(8,128)S(1)}, f32[8,64,128]{2,1,0:T(8,128)}, f32[8,64,128]{2,1,0:T(8,...) fusion(f32[8,64,128]{2,1,0:T(8,128)} %get-tuple-element.1309, s32[]{:T(128)S(6)} %copy.408, ...), kind=kLoop, calls=%fused_computation.clone.1 | loop fusion | flops 122880 | bytes 458757 | tf_op jit(solution)/shard_map/while/body/jit(dynamic_update_index_in_dim)/dynamic_update_slice | solution.py:103
  83.5 1.5 %bitcast_dynamic-update-slice_fusion.16 = (f32[8,64,128]{2,1,0:T(8,128)}, f32[64,128]{1,0:T(8,128)S(1)}, f32[8,64,128]{2,1,0:T(8,128)}, f32[8,64,128]{2,1,0:T(8,...) fusion(f32[8,64,128]{2,1,0:T(8,128)} %get-tuple-element.1309, s32[]{:T(128)S(6)} %copy.408, ...), kind=kLoop, calls=%fused_computation.clone.1 | loop fusion | flops 122880 | bytes 458757 | tf_op jit(solution)/shard_map/while/body/jit(dynamic_update_index_in_dim)/dynamic_update_slice | solution.py:103
  85.0 1.5 %bitcast_dynamic-update-slice_fusion.16 = (f32[8,64,128]{2,1,0:T(8,128)}, f32[64,128]{1,0:T(8,128)S(1)}, f32[8,64,128]{2,1,0:T(8,128)}, f32[8,64,128]{2,1,0:T(8,...) fusion(f32[8,64,128]{2,1,0:T(8,128)} %get-tuple-element.1309, s32[]{:T(128)S(6)} %copy.408, ...), kind=kLoop, calls=%fused_computation.clone.1 | loop fusion | flops 122880 | bytes 458757 | tf_op jit(solution)/shard_map/while/body/jit(dynamic_update_index_in_dim)/dynamic_update_slice | solution.py:103
  87.9 11.6 %while.81 = (s32[]{:T(128)}, f32[64,128]{1,0:T(8,128)S(1)}, f32[8,64,128]{2,1,0:T(8,128)}, f32[8,64,128]{2,1,0:T(8,128)}, f32[8,64,128]{2,1,0:T(8,128)}, /*index...) while((s32[]{:T(128)}, f32[64,128]{1,0:T(8,128)S(1)}, ...), condition=%wide.region_3.4_spmd.clone, body=%wide.region_2.3_spmd.clone.sunk | while | flops 40964 | bytes 262287 | solution.py:111
  87.9 1.5 %bitcast_dynamic-update-slice_fusion.17 = (f32[8,64,128]{2,1,0:T(8,128)}, f32[64,128]{1,0:T(8,128)S(1)}, f32[8,64,128]{2,1,0:T(8,128)}) fusion(f32[8,64,128]{2,1,0:T(8,128)} %get-tuple-element.1346, s32[]{:T(128)S(6)} %sub.273, f32[64,128]{1,0:T(8,128)S(1)} %get-tuple-element.1345, pred[]{:T(512)S(6)} %compare.143, ...), kind=kLoop, calls=%fused_computation.18.clone.1 | loop fusion | flops 40960 | bytes 262149 | tf_op jit(solution)/shard_map/while/body/jit(dynamic_update_index_in_dim)/dynamic_update_slice | solution.py:103
  90.8 1.5 %bitcast_dynamic-update-slice_fusion.17 = (f32[8,64,128]{2,1,0:T(8,128)}, f32[64,128]{1,0:T(8,128)S(1)}, f32[8,64,128]{2,1,0:T(8,128)}) fusion(f32[8,64,128]{2,1,0:T(8,128)} %get-tuple-element.1346, s32[]{:T(128)S(6)} %sub.273, f32[64,128]{1,0:T(8,128)S(1)} %get-tuple-element.1345, pred[]{:T(512)S(6)} %compare.143, ...), kind=kLoop, calls=%fused_computation.18.clone.1 | loop fusion | flops 40960 | bytes 262149 | tf_op jit(solution)/shard_map/while/body/jit(dynamic_update_index_in_dim)/dynamic_update_slice | solution.py:103
  92.3 1.4 %bitcast_dynamic-update-slice_fusion.17 = (f32[8,64,128]{2,1,0:T(8,128)}, f32[64,128]{1,0:T(8,128)S(1)}, f32[8,64,128]{2,1,0:T(8,128)}) fusion(f32[8,64,128]{2,1,0:T(8,128)} %get-tuple-element.1346, s32[]{:T(128)S(6)} %sub.273, f32[64,128]{1,0:T(8,128)S(1)} %get-tuple-element.1345, pred[]{:T(512)S(6)} %compare.143, ...), kind=kLoop, calls=%fused_computation.18.clone.1 | loop fusion | flops 40960 | bytes 262149 | tf_op jit(solution)/shard_map/while/body/jit(dynamic_update_index_in_dim)/dynamic_update_slice | solution.py:103
  93.7 1.4 %bitcast_dynamic-update-slice_fusion.17 = (f32[8,64,128]{2,1,0:T(8,128)}, f32[64,128]{1,0:T(8,128)S(1)}, f32[8,64,128]{2,1,0:T(8,128)}) fusion(f32[8,64,128]{2,1,0:T(8,128)} %get-tuple-element.1346, s32[]{:T(128)S(6)} %sub.273, f32[64,128]{1,0:T(8,128)S(1)} %get-tuple-element.1345, pred[]{:T(512)S(6)} %compare.143, ...), kind=kLoop, calls=%fused_computation.18.clone.1 | loop fusion | flops 40960 | bytes 262149 | tf_op jit(solution)/shard_map/while/body/jit(dynamic_update_index_in_dim)/dynamic_update_slice | solution.py:103
  95.2 1.5 %bitcast_dynamic-update-slice_fusion.17 = (f32[8,64,128]{2,1,0:T(8,128)}, f32[64,128]{1,0:T(8,128)S(1)}, f32[8,64,128]{2,1,0:T(8,128)}) fusion(f32[8,64,128]{2,1,0:T(8,128)} %get-tuple-element.1346, s32[]{:T(128)S(6)} %sub.273, f32[64,128]{1,0:T(8,128)S(1)} %get-tuple-element.1345, pred[]{:T(512)S(6)} %compare.143, ...), kind=kLoop, calls=%fused_computation.18.clone.1 | loop fusion | flops 40960 | bytes 262149 | tf_op jit(solution)/shard_map/while/body/jit(dynamic_update_index_in_dim)/dynamic_update_slice | solution.py:103
  96.6 1.4 %bitcast_dynamic-update-slice_fusion.17 = (f32[8,64,128]{2,1,0:T(8,128)}, f32[64,128]{1,0:T(8,128)S(1)}, f32[8,64,128]{2,1,0:T(8,128)}) fusion(f32[8,64,128]{2,1,0:T(8,128)} %get-tuple-element.1346, s32[]{:T(128)S(6)} %sub.273, f32[64,128]{1,0:T(8,128)S(1)} %get-tuple-element.1345, pred[]{:T(512)S(6)} %compare.143, ...), kind=kLoop, calls=%fused_computation.18.clone.1 | loop fusion | flops 40960 | bytes 262149 | tf_op jit(solution)/shard_map/while/body/jit(dynamic_update_index_in_dim)/dynamic_update_slice | solution.py:103
  98.1 1.5 %bitcast_dynamic-update-slice_fusion.17 = (f32[8,64,128]{2,1,0:T(8,128)}, f32[64,128]{1,0:T(8,128)S(1)}, f32[8,64,128]{2,1,0:T(8,128)}) fusion(f32[8,64,128]{2,1,0:T(8,128)} %get-tuple-element.1346, s32[]{:T(128)S(6)} %sub.273, f32[64,128]{1,0:T(8,128)S(1)} %get-tuple-element.1345, pred[]{:T(512)S(6)} %compare.143, ...), kind=kLoop, calls=%fused_computation.18.clone.1 | loop fusion | flops 40960 | bytes 262149 | tf_op jit(solution)/shard_map/while/body/jit(dynamic_update_index_in_dim)/dynamic_update_slice | solution.py:103
  103.3 2.1 %multiply_add_fusion.24 = (f32[64,16,128]{2,0,1:T(8,128)S(1)}, f32[64,16,128]{2,0,1:T(8,128)S(1)}, f32[64,16,128]{2,0,1:T(8,128)S(1)}, f32[64,16,128]{2,0,1:T(8,...) fusion(f32[64,16,128]{2,0,1:T(8,128)S(1)} %copy-done.5, ...), kind=kLoop, calls=%fused_computation.141 | loop fusion | flops 2359296 | bytes 11476992 | tf_op jit(solution)/shard_map/add | solution.py:56
  121.5 13.8 %all-gather.1 = f32[24,64,16]{1,2,0:T(8,128)S(1)} all-gather(f32[6,64,16]{1,2,0:T(8,128)S(1)} %constant_dynamic-update-slice_fusion), channel_id=3, replica_groups=mesh['row'=8,'col'=4] {'col'}, dimensions={0}, use_global_device_ids=true | all-gather | bytes 122880 | tf_op jit(solution)/shard_map/all_gather | solution.py:165
  (202 shorter events, 54.5 us)
Async XLA Ops:
  6.5 62.6 %all-gather.4.cloned.1.call-start = ((), (), s32[]{:S(2)}) async-start(), calls=%async_computation | async-start | bytes 1769472 | tf_op jit(solution)/shard_map/all_gather | solution.py:152
  9.1 4.4 %collective-permute-start.1 = (f32[2,64,1,128]{3,1,2,0:T(8,128)S(1)}, f32[2,64,1,128]{3,1,2,0:T(8,128)S(1)}, u32[]{:S(2)}, u32[]{:S(2)}) collective-permute-start(f32[2,64,1,128]{3,1,2,0:T(8,128)S(1)} %get-tuple-element.851), channel_id=1, source_target_pairs={{4,0},{8,4},{12,8},{16,12},{20,16},{24,20},{28,24},{5,1},{9,5},{13... | collective-permute-start | bytes 196616 | tf_op jit(solution)/shard_map/ppermute | solution.py:17
  10.4 3.9 %collective-permute-start = (f32[2,64,1,128]{3,1,2,0:T(8,128)S(1)}, f32[2,64,1,128]{3,1,2,0:T(8,128)S(1)}, u32[]{:S(2)}, u32[]{:S(2)}) collective-permute-start(f32[2,64,1,128]{3,1,2,0:T(8,128)S(1)} %get-tuple-element.850), channel_id=1, source_target_pairs={{0,4},{4,8},{8,12},{12,16},{16,20},{20,24},{24,28},{1,5},{5,9},{9,... | collective-permute-start | bytes 196616 | tf_op jit(solution)/shard_map/ppermute | solution.py:14
  15.9 7.9 %collective-permute-start.3 = (f32[2,64,18,1]{1,0,3,2:T(2,128)}, f32[2,64,18,1]{1,0,3,2:T(2,128)S(1)}, u32[]{:S(2)}, u32[]{:S(2)}) collective-permute-start(f32[2,64,18,1]{1,0,3,2:T(2,128)} %copy.304), channel_id=1, source_target_pairs={{1,0},{2,1},{3,2},{5,4},{6,5},{7,6},{9,8},{10,9},{11,10},{13,12},{... | collective-permute-start | bytes 27656 | tf_op jit(solution)/shard_map/ppermute | solution.py:17
  17.6 7.0 %collective-permute-start.2 = (f32[2,64,18,1]{1,0,3,2:T(2,128)S(1)}, f32[2,64,18,1]{1,0,3,2:T(2,128)}, u32[]{:S(2)}, u32[]{:S(2)}) collective-permute-start(f32[2,64,18,1]{1,0,3,2:T(2,128)S(1)} %copy.303), channel_id=1, source_target_pairs={{0,1},{1,2},{2,3},{4,5},{5,6},{6,7},{8,9},{9,10},{10,11},{12,13},{... | collective-permute-start | bytes 27656 | tf_op jit(solution)/shard_map/ppermute | solution.py:14
  26.8 1.0 copy-start
  26.8 1.2 copy-start.19
  26.8 1.3 copy-start.20
  36.0 1.0 copy-start.10
  38.0 1.0 copy-start.1
  39.8 4.5 %copy-start.2 = (f32[64,16,128]{2,0,1:T(8,128)}, f32[64,16,128]{2,0,1:T(8,128)S(1)}, u32[]{:S(2)}) copy-start(f32[64,16,128]{2,0,1:T(8,128)S(1)} %get-tuple-element.745) | copy-start | bytes 1572868
  39.8 4.5 %copy-start.4 = (f32[64,16,128]{2,0,1:T(8,128)}, f32[64,16,128]{2,0,1:T(8,128)S(1)}, u32[]{:S(2)}) copy-start(f32[64,16,128]{2,0,1:T(8,128)S(1)} %get-tuple-element.747) | copy-start | bytes 1572868
  73.7 27.4 %copy-start.11 = (f32[64,16,128]{2,0,1:T(8,128)S(1)}, f32[64,16,128]{2,0,1:T(8,128)}, u32[]{:S(2)}) copy-start(f32[64,16,128]{2,0,1:T(8,128)} %copy-done.10) | copy-start | bytes 1572868
  74.4 26.7 %copy-start.9 = (f32[64,16,128]{2,0,1:T(8,128)S(1)}, f32[64,16,128]{2,0,1:T(8,128)}, u32[]{:S(2)}) copy-start(f32[64,16,128]{2,0,1:T(8,128)} %copy-done.8) | copy-start | bytes 1572868
  86.5 14.6 %copy-start.7 = (f32[64,16,128]{2,0,1:T(8,128)S(1)}, f32[64,16,128]{2,0,1:T(8,128)}, u32[]{:S(2)}) copy-start(f32[64,16,128]{2,0,1:T(8,128)} %copy-done.6) | copy-start | bytes 1572868
  101.1 1.0 copy-start.15
  101.1 1.2 copy-start.16
  101.1 1.3 copy-start.17
  101.1 1.5 %copy-start.18 = (f32[64,16,127]{2,0,1:T(8,128)S(1)}, f32[64,16,127]{2,0,1:T(8,128)}, u32[]{:S(2)}) copy-start(f32[64,16,127]{2,0,1:T(8,128)} %get-tuple-element.972) | copy-start | bytes 1560580
  101.2 1.5 %copy-start.3 = (f32[64,16,128]{2,0,1:T(8,128)S(1)}, f32[64,16,128]{2,0,1:T(8,128)}, u32[]{:S(2)}) copy-start(f32[64,16,128]{2,0,1:T(8,128)} %copy-done.2) | copy-start | bytes 1572868
  101.2 1.7 %copy-start.5 = (f32[64,16,128]{2,0,1:T(8,128)S(1)}, f32[64,16,128]{2,0,1:T(8,128)}, u32[]{:S(2)}) copy-start(f32[64,16,128]{2,0,1:T(8,128)} %copy-done.4) | copy-start | bytes 1572868
  101.3 1.8 %copy-start.13 = (f32[64,16,127]{2,0,1:T(8,128)S(1)}, f32[64,16,127]{2,0,1:T(8,128)}, u32[]{:S(2)}) copy-start(f32[64,16,127]{2,0,1:T(8,128)} %get-tuple-element.938) | copy-start | bytes 1560580
  101.3 2.0 %copy-start.14 = (f32[64,16,127]{2,0,1:T(8,128)S(1)}, f32[64,16,127]{2,0,1:T(8,128)}, u32[]{:S(2)}) copy-start(f32[64,16,127]{2,0,1:T(8,128)} %get-tuple-element.939) | copy-start | bytes 1560580
  121.5 14.4 %copy-start.12 = (f32[64,16,128]{2,1,0:T(8,128)S(1)}, f32[64,16,128]{2,1,0:T(8,128)}, u32[]{:S(2)}) copy-start(f32[64,16,128]{2,1,0:T(8,128)} %param.10) | copy-start | bytes 1572868
  (3 other events, 2.3 us)
Sparse Core Ops, SparseCore 0:
  37.9 31.1 all-gather.3
where the time goes:
time: 146 us; the launch traced here: 144 us
  other arithmetic  43.1 us (30%)
  local copies, waits for them, and re-layouts  36.4 us (25%)
  waiting for transfers between devices  24.6 us (17%)
  between operations  14.2 us (10%)
  blocking collectives  13.8 us (9%)
  starting transfers between devices  11.8 us (8%)
    dynamic_update_slice x24, other arithmetic, join_spikes(): unused, outputs = lax.scan(forward, (zero_plane, zero_plane), columns_in)  23.8 us
    all_gather x1, waiting for transfers between devices, on_device(): gathered = lax.all_gather(planes, 'row', axis=0, tiled=True)  23.3 us
    all_gather x1, blocking collectives, on_device(): gathered = lax.all_gather(planes, 'col', axis=0, tiled=True)  13.8 us
    add x11, other arithmetic, reduce_lines(): column + left_factor * shifted(column, line_axis, stride, 0.0)  10.7 us
    slice x41, local copies, waits for them, and re-layouts, shifted(): kept_part = lax.slice_in_dim(values, 0, length - stride, axis=line_axis)  9.44 us
    ppermute x2, starting transfers between devices, padded_2(): lax.ppermute(lax.slice_in_dim(block, block.shape[dim] - width, None, axis...  9.22 us
    unnamed x55, local copies, waits for them, and re-layouts  8.25 us
    slice x24, local copies, waits for them, and re-layouts, shifted(): kept_part = lax.slice_in_dim(values, -stride, length, axis=line_axis)  5.6 us
  transfers between devices with their start and end apart: 5, of which 3 were waited for; matrix products, arithmetic and copies ran while one was open for 6% of the time, Pallas kernels for 0%

commit v1 on v0

--- a/solution.py
+++ b/solution.py
@@ -162,7 +162,12 @@
     local_part, left_spike, right_spike, planes = local_spikes(
         -west_ydir, -east_ydir, delta_xdir, 2
     )
-    gathered = lax.all_gather(planes, "col", axis=0, tiled=True)
+    ring = [planes]
+    for hop in range(3):
+        ring.append(lax.ppermute(ring[-1], "col", [(dev, (dev + 1) % 4) for dev in range(4)]))
+    gathered = jnp.roll(
+        jnp.concatenate(ring[::-1], axis=0), (lax.axis_index("col") + 1) * ring[0].shape[0], axis=0
+    )
     delta_ydir = join_spikes(
         gathered,
         local_part,

time: 146 us -> 150 us (1.027)
  waiting for transfers between devices: 24.6 us -> 40.9 us
  blocking collectives: 13.8 us -> 0 us
  starting transfers between devices: 11.8 us -> 13.3 us
    ppermute x0 -> x3, waiting for transfers between devices: none -> 16.2 us  [on_device(): lax.ppermute(ring[-1], 'col', [(dev, (dev + 1) % 4) for dev in range(4)])]
    all_gather x1 -> x0, blocking collectives: 13.8 us -> none  [on_device(): gathered = lax.all_gather(planes, 'col', axis=0, tiled=True)]
    ppermute x0 -> x3, starting transfers between devices: none -> 1.54 us  [on_device(): lax.ppermute(ring[-1], 'col', [(dev, (dev + 1) % 4) for dev in range(4)])]
    unnamed x55 -> x62, local copies, waits for them, and re-layouts: 8.25 us -> 8.75 us
  transfers between devices with their start and end apart: 5 -> 8, of which waited for: 3 -> 6; matrix products, arithmetic and copies ran while one was open for 6% -> 5% of each run, Pallas kernels for 0% -> 0%
where the time goes in v1:
time: 150 us; the launch traced here: 148 us
  other arithmetic  42.8 us (29%)
  waiting for transfers between devices  40.9 us (27%)
  local copies, waits for them, and re-layouts  36.8 us (25%)
  between operations  14.3 us (10%)
  starting transfers between devices  13.3 us (9%)
    dynamic_update_slice x24, other arithmetic, join_spikes(): unused, outputs = lax.scan(forward, (zero_plane, zero_plane), columns_in)  23.5 us
    all_gather x1, waiting for transfers between devices, on_device(): gathered = lax.all_gather(planes, 'row', axis=0, tiled=True)  23.4 us
    ppermute x3, waiting for transfers between devices, on_device(): lax.ppermute(ring[-1], 'col', [(dev, (dev + 1) % 4) for dev in range(4)])  16.2 us
    add x11, other arithmetic, reduce_lines(): column + left_factor * shifted(column, line_axis, stride, 0.0)  10.7 us
    slice x41, local copies, waits for them, and re-layouts, shifted(): kept_part = lax.slice_in_dim(values, 0, length - stride, axis=line_axis)  9.37 us
    ppermute x2, starting transfers between devices, padded_2(): lax.ppermute(lax.slice_in_dim(block, block.shape[dim] - width, None, axis...  9.22 us
    unnamed x62, local copies, waits for them, and re-layouts  8.75 us
    slice x24, local copies, waits for them, and re-layouts, shifted(): kept_part = lax.slice_in_dim(values, -stride, length, axis=line_axis)  5.57 us
  transfers between devices with their start and end apart: 8, of which 6 were waited for; matrix products, arithmetic and copies ran while one was open for 5% of the time, Pallas kernels for 0%

profile of v1, /device:TPU:0, one launch (start us, length us, event | category | flops | bytes accessed | tf_op | source)
XLA Modules:
  0.0 148.4 jit_solution(16717474656156676164)
XLA Ops:
  6.5 2.5 %fusion.53 = (f32[64,16,128]{2,0,1:T(8,128)}, f32[1,64,16,128]{3,1,2,0:T(8,128)S(1)}, f32[1,64,16,128]{3,1,2,0:T(8,128)S(1)}, f32[64,16,128]{2,0,1:T(8,128)}) fusion(f32[64,16,128]{2,1,0:T(8,128)} %param.10, f32[64,16,128]{2,1,0:T(8,128)} %param.11), kind=kLoop, calls=%fused_computation.249 | loop fusion | bytes 3145728 | tf_op args[0]
  10.4 3.0 %collective-permute-start = (f32[2,64,1,128]{3,1,2,0:T(8,128)S(1)}, f32[2,64,1,128]{3,1,2,0:T(8,128)S(1)}, u32[]{:S(2)}, u32[]{:S(2)}) collective-permute-start(f32[2,64,1,128]{3,1,2,0:T(8,128)S(1)} %get-tuple-element.863), channel_id=1, source_target_pairs={{0,4},{4,8},{8,12},{12,16},{16,20},{20,24},{24,28},{1,5},{5,9},{9,... | collective-permute-start | bytes 196616 | tf_op jit(solution)/shard_map/ppermute | solution.py:14
  17.6 6.2 %collective-permute-start.2 = (f32[2,64,18,1]{1,0,3,2:T(2,128)S(1)}, f32[2,64,18,1]{1,0,3,2:T(2,128)}, u32[]{:S(2)}, u32[]{:S(2)}) collective-permute-start(f32[2,64,18,1]{1,0,3,2:T(2,128)S(1)} %copy.267), channel_id=1, source_target_pairs={{0,1},{1,2},{2,3},{4,5},{5,6},{6,7},{8,9},{9,10},{10,11},{12,13},{... | collective-permute-start | bytes 27656 | tf_op jit(solution)/shard_map/ppermute | solution.py:14
  45.6 23.4 %all-gather.3.cloned.1.call-done = f32[48,64,128]{2,1,0:T(8,128)} async-done(((f32[6,64,128]{2,1,0:T(8,128)}), f32[48,64,128]{2,1,0:T(8,128)}) %all-gather.3.cloned.1.call-update) | async-done | bytes 1572880 | tf_op jit(solution)/shard_map/all_gather | solution.py:152
  69.1 2.4 %slice_bitcast_fusion.2 = (f32[8,64,128]{2,1,0:T(8,128)S(1)}, f32[8,64,128]{2,1,0:T(8,128)S(1)}, f32[8,64,128]{2,1,0:T(8,128)}, f32[8,64,128]{2,1,0:T(8,128)}, f32[8,64,128]{2,1,0:T(8,128)}, /*index=5*/f32[8,64,128]{2,1,0:T(8,128)}) fusion(f32[8,6,64,128]{3,2,1,0:T(8,128)} %bitcast.271), kind=kLoop, calls=%fused_computation.177 | loop fusion | bytes 3145728 | tf_op jit(solution)/shard_map/squeeze | solution.py:90
  74.4 11.9 %while.80 = (s32[]{:T(128)}, f32[64,128]{1,0:T(8,128)S(1)}, f32[64,128]{1,0:T(8,128)S(1)}, f32[8,64,128]{2,1,0:T(8,128)}, f32[8,64,128]{2,1,0:T(8,128)}, /*index...) while((s32[]{:T(128)}, f32[64,128]{1,0:T(8,128)S(1)}, ...), condition=%wide.region_1.2_spmd.clone, body=%wide.region_0.1_spmd.clone.sunk | while | flops 122883 | bytes 458915 | solution.py:103
  74.4 1.6 %bitcast_dynamic-update-slice_fusion.16 = (f32[8,64,128]{2,1,0:T(8,128)}, f32[64,128]{1,0:T(8,128)S(1)}, f32[8,64,128]{2,1,0:T(8,128)}, f32[8,64,128]{2,1,0:T(8,...) fusion(f32[8,64,128]{2,1,0:T(8,128)} %get-tuple-element.1322, s32[]{:T(128)S(6)} %copy.360, ...), kind=kLoop, calls=%fused_computation.clone.1 | loop fusion | flops 122880 | bytes 458757 | tf_op jit(solution)/shard_map/while/body/jit(dynamic_update_index_in_dim)/dynamic_update_slice | solution.py:103
  75.9 1.5 bitcast_dynamic-update-slice_fusion.16
  77.4 1.5 bitcast_dynamic-update-slice_fusion.16
  78.9 1.5 bitcast_dynamic-update-slice_fusion.16
  80.3 1.5 bitcast_dynamic-update-slice_fusion.16
  81.8 1.5 bitcast_dynamic-update-slice_fusion.16
  83.3 1.5 %bitcast_dynamic-update-slice_fusion.16 = (f32[8,64,128]{2,1,0:T(8,128)}, f32[64,128]{1,0:T(8,128)S(1)}, f32[8,64,128]{2,1,0:T(8,128)}, f32[8,64,128]{2,1,0:T(8,...) fusion(f32[8,64,128]{2,1,0:T(8,128)} %get-tuple-element.1322, s32[]{:T(128)S(6)} %copy.360, ...), kind=kLoop, calls=%fused_computation.clone.1 | loop fusion | flops 122880 | bytes 458757 | tf_op jit(solution)/shard_map/while/body/jit(dynamic_update_index_in_dim)/dynamic_update_slice | solution.py:103
  84.8 1.5 bitcast_dynamic-update-slice_fusion.16
  87.7 11.5 %while.81 = (s32[]{:T(128)}, f32[64,128]{1,0:T(8,128)S(1)}, f32[8,64,128]{2,1,0:T(8,128)}, f32[8,64,128]{2,1,0:T(8,128)}, f32[8,64,128]{2,1,0:T(8,128)}, /*index...) while((s32[]{:T(128)}, f32[64,128]{1,0:T(8,128)S(1)}, ...), condition=%wide.region_3.4_spmd.clone, body=%wide.region_2.3_spmd.clone.sunk | while | flops 40964 | bytes 262287 | solution.py:111
  89.2 1.5 bitcast_dynamic-update-slice_fusion.17
  90.6 1.4 bitcast_dynamic-update-slice_fusion.17
  92.1 1.4 bitcast_dynamic-update-slice_fusion.17
  94.9 1.4 bitcast_dynamic-update-slice_fusion.17
  103.0 2.1 %multiply_add_fusion.24 = (f32[64,16,128]{2,0,1:T(8,128)S(1)}, f32[64,16,128]{2,0,1:T(8,128)S(1)}, f32[64,16,128]{2,0,1:T(8,128)S(1)}, f32[64,16,128]{2,0,1:T(8,...) fusion(f32[64,16,128]{2,0,1:T(8,128)S(1)} %copy-done.5, ...), kind=kLoop, calls=%fused_computation.141 | loop fusion | flops 2359296 | bytes 11476992 | tf_op jit(solution)/shard_map/add | solution.py:56
  121.2 1.5 %collective-permute-start.4 = (f32[1,6,64,16]{2,3,1,0:T(8,128)S(1)}, f32[1,6,64,16]{2,3,1,0:T(8,128)S(1)}, u32[]{:S(2)}, u32[]{:S(2)}) collective-permute-start(f32[1,6,64,16]{2,3,1,0:T(8,128)S(1)} %bitcast.272), channel_id=1, source_target_pairs={{0,1},{1,2},{2,3},{3,0},{4,5},{5,6},{6,7},{7,4},{8,9},{9,10},{10,1... | collective-permute-start | bytes 73736 | tf_op jit(solution)/shard_map/ppermute | solution.py:167
  122.8 4.4 %collective-permute-done.4 = f32[1,6,64,16]{2,3,1,0:T(8,128)S(1)} collective-permute-done((f32[1,6,64,16]{2,3,1,0:T(8,128)S(1)}, f32[1,6,64,16]{2,3,1,0:T(8,128)S(1)}, u32[]{:S(2)}, u32[]{:S(2)}) %collective-permute-start.4) | collective-permute-done | bytes 24608 | tf_op jit(solution)/shard_map/ppermute | solution.py:167
  127.2 5.9 %collective-permute-done.5 = f32[1,6,64,16]{2,3,1,0:T(8,128)S(1)} collective-permute-done((f32[1,6,64,16]{2,3,1,0:T(8,128)S(1)}, f32[1,6,64,16]{2,3,1,0:T(8,128)S(1)}, u32[]{:S(2)}, u32[]{:S(2)}) %collective-permute-start.5) | collective-permute-done | bytes 24608 | tf_op jit(solution)/shard_map/ppermute | solution.py:167
  133.1 5.9 %collective-permute-done.6 = f32[1,6,64,16]{2,3,1,0:T(8,128)S(1)} collective-permute-done((f32[1,6,64,16]{2,3,1,0:T(8,128)S(1)}, f32[1,6,64,16]{2,3,1,0:T(8,128)S(1)}, u32[]{:S(2)}, u32[]{:S(2)}) %collective-permute-start.6) | collective-permute-done | bytes 24608 | tf_op jit(solution)/shard_map/ppermute | solution.py:167
  (215 shorter events, 59.2 us)
Async XLA Ops:
  6.5 62.5 %all-gather.3.cloned.1.call-start = ((), (), s32[]{:S(2)}) async-start(), calls=%async_computation | async-start | bytes 1769472 | tf_op jit(solution)/shard_map/all_gather | solution.py:152
  9.1 4.4 %collective-permute-start.1 = (f32[2,64,1,128]{3,1,2,0:T(8,128)S(1)}, f32[2,64,1,128]{3,1,2,0:T(8,128)S(1)}, u32[]{:S(2)}, u32[]{:S(2)}) collective-permute-start(f32[2,64,1,128]{3,1,2,0:T(8,128)S(1)} %get-tuple-element.864), channel_id=1, source_target_pairs={{4,0},{8,4},{12,8},{16,12},{20,16},{24,20},{28,24},{5,1},{9,5},{13... | collective-permute-start | bytes 196616 | tf_op jit(solution)/shard_map/ppermute | solution.py:17
  10.4 3.9 %collective-permute-start = (f32[2,64,1,128]{3,1,2,0:T(8,128)S(1)}, f32[2,64,1,128]{3,1,2,0:T(8,128)S(1)}, u32[]{:S(2)}, u32[]{:S(2)}) collective-permute-start(f32[2,64,1,128]{3,1,2,0:T(8,128)S(1)} %get-tuple-element.863), channel_id=1, source_target_pairs={{0,4},{4,8},{8,12},{12,16},{16,20},{20,24},{24,28},{1,5},{5,9},{9,... | collective-permute-start | bytes 196616 | tf_op jit(solution)/shard_map/ppermute | solution.py:14
  15.9 7.9 %collective-permute-start.3 = (f32[2,64,18,1]{1,0,3,2:T(2,128)}, f32[2,64,18,1]{1,0,3,2:T(2,128)S(1)}, u32[]{:S(2)}, u32[]{:S(2)}) collective-permute-start(f32[2,64,18,1]{1,0,3,2:T(2,128)} %copy.268), channel_id=1, source_target_pairs={{1,0},{2,1},{3,2},{5,4},{6,5},{7,6},{9,8},{10,9},{11,10},{13,12},{... | collective-permute-start | bytes 27656 | tf_op jit(solution)/shard_map/ppermute | solution.py:17
  17.6 7.0 %collective-permute-start.2 = (f32[2,64,18,1]{1,0,3,2:T(2,128)S(1)}, f32[2,64,18,1]{1,0,3,2:T(2,128)}, u32[]{:S(2)}, u32[]{:S(2)}) collective-permute-start(f32[2,64,18,1]{1,0,3,2:T(2,128)S(1)} %copy.267), channel_id=1, source_target_pairs={{0,1},{1,2},{2,3},{4,5},{5,6},{6,7},{8,9},{9,10},{10,11},{12,13},{... | collective-permute-start | bytes 27656 | tf_op jit(solution)/shard_map/ppermute | solution.py:14
  26.8 1.0 copy-start
  26.8 1.2 copy-start.19
  26.8 1.3 copy-start.20
  38.0 1.0 copy-start.1
  39.7 4.4 %copy-start.2 = (f32[64,16,128]{2,0,1:T(8,128)}, f32[64,16,128]{2,0,1:T(8,128)S(1)}, u32[]{:S(2)}) copy-start(f32[64,16,128]{2,0,1:T(8,128)S(1)} %get-tuple-element.758) | copy-start | bytes 1572868
  39.7 4.4 %copy-start.4 = (f32[64,16,128]{2,0,1:T(8,128)}, f32[64,16,128]{2,0,1:T(8,128)S(1)}, u32[]{:S(2)}) copy-start(f32[64,16,128]{2,0,1:T(8,128)S(1)} %get-tuple-element.760) | copy-start | bytes 1572868
  73.7 27.1 %copy-start.11 = (f32[64,16,128]{2,0,1:T(8,128)S(1)}, f32[64,16,128]{2,0,1:T(8,128)}, u32[]{:S(2)}) copy-start(f32[64,16,128]{2,0,1:T(8,128)} %copy-done.10) | copy-start | bytes 1572868
  74.4 26.4 %copy-start.9 = (f32[64,16,128]{2,0,1:T(8,128)S(1)}, f32[64,16,128]{2,0,1:T(8,128)}, u32[]{:S(2)}) copy-start(f32[64,16,128]{2,0,1:T(8,128)} %copy-done.8) | copy-start | bytes 1572868
  86.3 14.5 %copy-start.7 = (f32[64,16,128]{2,0,1:T(8,128)S(1)}, f32[64,16,128]{2,0,1:T(8,128)}, u32[]{:S(2)}) copy-start(f32[64,16,128]{2,0,1:T(8,128)} %copy-done.6) | copy-start | bytes 1572868
  100.8 1.2 copy-start.16
  100.8 1.3 copy-start.17
  100.8 1.5 %copy-start.18 = (f32[64,16,127]{2,0,1:T(8,128)S(1)}, f32[64,16,127]{2,0,1:T(8,128)}, u32[]{:S(2)}) copy-start(f32[64,16,127]{2,0,1:T(8,128)} %get-tuple-element.985) | copy-start | bytes 1560580
  101.0 1.5 %copy-start.3 = (f32[64,16,128]{2,0,1:T(8,128)S(1)}, f32[64,16,128]{2,0,1:T(8,128)}, u32[]{:S(2)}) copy-start(f32[64,16,128]{2,0,1:T(8,128)} %copy-done.2) | copy-start | bytes 1572868
  101.0 1.7 %copy-start.5 = (f32[64,16,128]{2,0,1:T(8,128)S(1)}, f32[64,16,128]{2,0,1:T(8,128)}, u32[]{:S(2)}) copy-start(f32[64,16,128]{2,0,1:T(8,128)} %copy-done.4) | copy-start | bytes 1572868
  101.0 1.8 %copy-start.13 = (f32[64,16,127]{2,0,1:T(8,128)S(1)}, f32[64,16,127]{2,0,1:T(8,128)}, u32[]{:S(2)}) copy-start(f32[64,16,127]{2,0,1:T(8,128)} %get-tuple-element.951) | copy-start | bytes 1560580
  101.0 2.0 %copy-start.14 = (f32[64,16,127]{2,0,1:T(8,128)S(1)}, f32[64,16,127]{2,0,1:T(8,128)}, u32[]{:S(2)}) copy-start(f32[64,16,127]{2,0,1:T(8,128)} %get-tuple-element.952) | copy-start | bytes 1560580
  121.2 5.9 %collective-permute-start.4 = (f32[1,6,64,16]{2,3,1,0:T(8,128)S(1)}, f32[1,6,64,16]{2,3,1,0:T(8,128)S(1)}, u32[]{:S(2)}, u32[]{:S(2)}) collective-permute-start(f32[1,6,64,16]{2,3,1,0:T(8,128)S(1)} %bitcast.272), channel_id=1, source_target_pairs={{0,1},{1,2},{2,3},{3,0},{4,5},{5,6},{6,7},{7,4},{8,9},{9,10},{10,1... | collective-permute-start | bytes 73736 | tf_op jit(solution)/shard_map/ppermute | solution.py:167
  127.2 5.9 %collective-permute-start.5 = (f32[1,6,64,16]{2,3,1,0:T(8,128)S(1)}, f32[1,6,64,16]{2,3,1,0:T(8,128)S(1)}, u32[]{:S(2)}, u32[]{:S(2)}) collective-permute-start(f32[1,6,64,16]{2,3,1,0:T(8,128)S(1)} %collective-permute-done.4), channel_id=1, source_target_pairs={{0,1},{1,2},{2,3},{3,0},{4,5},{5,6},{6,7},{7,4},{8,9},{9,10},{10,1... | collective-permute-start | bytes 73736 | tf_op jit(solution)/shard_map/ppermute | solution.py:167
  133.1 5.9 %collective-permute-start.6 = (f32[1,6,64,16]{2,3,1,0:T(8,128)S(1)}, f32[1,6,64,16]{2,3,1,0:T(8,128)S(1)}, u32[]{:S(2)}, u32[]{:S(2)}) collective-permute-start(f32[1,6,64,16]{2,3,1,0:T(8,128)S(1)} %collective-permute-done.5), channel_id=1, source_target_pairs={{0,1},{1,2},{2,3},{3,0},{4,5},{5,6},{6,7},{7,4},{8,9},{9,10},{10,1... | collective-permute-start | bytes 73736 | tf_op jit(solution)/shard_map/ppermute | solution.py:167
  (6 other events, 5.3 us)
Sparse Core Ops, SparseCore 0:
  37.8 31.1 all-gather.2
